TPU v7x, 32 devices: a whole 2x2x4 slice. The times are simulated.
32 devices in a mesh: node: 16 (over z, x, core), col: 2 (over y).
Axes of the slice: x: 2, y: 2, z: 4, core: 2. Of those that a mesh axis runs over, the one named last changes fastest.
Arguments:
- coefficients: bfloat16 [64, 256, 2048], P('node', None, 'col'), may hold values from -6 to 6
- transfer: bfloat16 [3, 64, 4, 256, 256], P(None, 'node', None, 'col'), may hold values from -0.1875 to 0.1875
Outputs:
- result: bfloat16 [64, 256, 2048], P('node', None, 'col')
All inputs are finite; a program needn't handle non-finite values.
Results may differ from a plain program's by a relative error of at most 0.0058.
Values may be sent and summed in bfloat16 or wider, within the bound.
A program may use at most 64 MiB of HBM per device.

v0:
```python
import jax
import jax.numpy as jnp
from jax import lax
from jax.sharding import PartitionSpec as P


def from_partner(array, axis, apart):
    return lax.ppermute(array, axis, [(i, i ^ 1 << apart) for i in range(lax.axis_size(axis))])


def local(coefficients, transfer):
    position = lax.axis_index("node")
    current = coefficients
    for level_index in range(3):
        weights_now = transfer[level_index]
        if level_index == 0:
            operand = current[:, None]
            form = "lers,emsc->lrc"
        else:
            bit_base = 2 * (level_index - 1)
            own_digit = position // 4 ** (level_index - 1) % 4
            partner_one = from_partner(current, "node", bit_base)
            partner_two, partner_three = from_partner((current, partner_one), "node", bit_base + 1)
            operand = jnp.stack([current, partner_one, partner_two, partner_three])
            order_idx = jnp.bitwise_xor(jnp.arange(4, dtype=jnp.int32), own_digit)
            weights_now = jnp.take(weights_now, order_idx, axis=1)
            form = "lers,elsc->lrc"
        mixed = jnp.einsum(
            form,
            lax.all_gather(weights_now, "col", axis=2, tiled=True),
            operand,
            preferred_element_type=jnp.float32,
        )
        current = mixed.astype(jnp.bfloat16)
    return current


def solution(mesh):
    return jax.shard_map(
        local,
        mesh=mesh,
        in_specs=(P("node", None, "col"), P(None, "node", None, "col", None)),
        out_specs=P("node", None, "col"),
        check_vma=False,
    )
```

profile of v0, /device:TPU:0, one launch (start us, length us, event | category | flops | bytes accessed | tf_op | source)
XLA Modules:
  0.0 354.8 jit_solution(14040748880440781067)
XLA Ops:
  6.5 0.0 copy-start
  6.5 0.0 all-gather.9.cloned.1.call-start
  6.5 3.8 %fusion.12 = (bf16[1,4,4,128,256]{4,3,2,1,0:T(8,128)(2,1)}, bf16[4,4,128,256]{3,2,1,0:T(8,128)(2,1)}, bf16[4,4,128,256]{3,2,1,0:T(8,128)(2,1)}) fusion(bf16[3,4,4,128,256]{4,3,2,1,0:T(8,128)(2,1)} %param.5), kind=kLoop, calls=%fused_computation.25 | loop fusion | bytes 6291456 | tf_op jit(solution)/shard_map/slice | solution.py:15
  10.3 0.0 all-gather.9.cloned.1.call-update
  10.3 0.0 all-gather.7.cloned.1.call-start
  10.4 35.9 %all-gather.9.cloned.1.call-done = bf16[1,4,4,256,256]{4,3,2,1,0:T(8,128)(2,1)} async-done(((bf16[1,4,4,128,256]{4,3,2,1,0:T(8,128)(2,1)}), bf16[1,4,4,256,256]{4,3,2,1,0:T(8,128)(2,1)}) %all-gather.9.cloned.1.call-update) | async-done | bytes 2097168 | tf_op jit(solution)/shard_map/all_gather | solution.py:30
  46.3 0.0 copy-done
  46.3 5.2 %bitcast_convert_fusion.2 = bf16[4,256,1024]{2,1,0:T(8,128)(2,1)} fusion(bf16[4,256,1024]{2,1,0:T(8,128)(2,1)S(1)} %copy-done, bf16[1,4,4,256,256]{4,3,2,1,0:T(8,128)(2,1)} %all-gather.9.cloned.1.call-done), kind=kOutput, calls=%fused_computation.10 | convolution fusion | flops 2148532224 | bytes 6291456 | tf_op jit(solution)/shard_map/lers,emsc->lrc/dot_general | solution.py:28
  51.6 0.0 collective-permute-start
  51.6 1.8 gather_fusion.1
  53.4 1.1 fusion.10
  54.6 0.0 all-gather.7.cloned.1.call-update
  54.6 0.0 all-gather.5.cloned.1.call-start
  54.6 1.5 collective-permute-start.1
  56.2 0.0 collective-permute-done
  56.2 1.3 collective-permute-start.2
  57.5 30.5 %all-gather.7.cloned.1.call-done = bf16[4,4,256,256]{3,2,1,0:T(8,128)(2,1)} async-done(((bf16[4,4,128,256]{3,2,1,0:T(8,128)(2,1)}), bf16[4,4,256,256]{3,2,1,0:T(8,128)(2,1)}) %all-gather.7.cloned.1.call-update) | async-done | bytes 2097168 | tf_op jit(solution)/shard_map/all_gather | solution.py:30
  88.0 15.5 %collective-permute-done.1 = bf16[4,256,1024]{2,1,0:T(8,128)(2,1)} collective-permute-done((bf16[4,256,1024]{2,1,0:T(8,128)(2,1)}, bf16[4,256,1024]{2,1,0:T(8,128)(2,1)}, u32[]{:S(2)}, u32[]{:S(2)}) %collective-permute-start.1) | collective-permute-done | bytes 2097184 | tf_op jit(solution)/shard_map/ppermute | solution.py:8
  103.5 44.5 %collective-permute-done.2 = bf16[4,256,1024]{2,1,0:T(8,128)(2,1)} collective-permute-done((bf16[4,256,1024]{2,1,0:T(8,128)(2,1)}, bf16[4,256,1024]{2,1,0:T(8,128)(2,1)}, u32[]{:S(2)}, u32[]{:S(2)}) %collective-permute-start.2) | collective-permute-done | bytes 2097184 | tf_op jit(solution)/shard_map/ppermute | solution.py:8
  148.0 6.4 %bitcast_convert_fusion.1 = bf16[4,256,1024]{2,1,0:T(8,128)(2,1)} fusion(bf16[4,4,256,256]{3,2,1,0:T(8,128)(2,1)} %all-gather.7.cloned.1.call-done, bf16[1,4,256,1024]{3,2,1,0:T(8,128)(2,1)} %bitcast.11, bf16[1,4,256,1024]{3,2,1,0:T(8,128)(2,1)} %bitcast.10, bf16[1,4,256,1024]{3,2,1,0:T(8,128)(2,1)} %bitcast.9, bf16[1,4,256,1024]{3,2,1,0:T(8,128)(2,1)} %bitcast.8), kind=kOutput, calls=%fused_computation.9 | convolution fusion | flops 2161115136 | bytes 12582912 | tf_op jit(solution)/shard_map/lers,elsc->lrc/dot_general | solution.py:28
  154.4 1.5 collective-permute-start.3
  155.9 1.8 gather_fusion
  157.8 1.1 fusion.11
  158.9 0.0 all-gather.5.cloned.1.call-update
  158.9 2.5 collective-permute-start.4
  161.4 82.2 %collective-permute-done.3 = bf16[4,256,1024]{2,1,0:T(8,128)(2,1)} collective-permute-done((bf16[4,256,1024]{2,1,0:T(8,128)(2,1)}, bf16[4,256,1024]{2,1,0:T(8,128)(2,1)}, u32[]{:S(2)}, u32[]{:S(2)}) %collective-permute-start.3) | collective-permute-done | bytes 2097184 | tf_op jit(solution)/shard_map/ppermute | solution.py:8
  243.5 0.5 collective-permute-start.5
  244.0 0.0 all-gather.5.cloned.1.call-done
  244.0 54.6 %collective-permute-done.4 = bf16[4,256,1024]{2,1,0:T(8,128)(2,1)} collective-permute-done((bf16[4,256,1024]{2,1,0:T(8,128)(2,1)}, bf16[4,256,1024]{2,1,0:T(8,128)(2,1)}, u32[]{:S(2)}, u32[]{:S(2)}) %collective-permute-start.4) | collective-permute-done | bytes 2097184 | tf_op jit(solution)/shard_map/ppermute | solution.py:8
  298.6 43.4 %collective-permute-done.5 = bf16[4,256,1024]{2,1,0:T(8,128)(2,1)} collective-permute-done((bf16[4,256,1024]{2,1,0:T(8,128)(2,1)}, bf16[4,256,1024]{2,1,0:T(8,128)(2,1)}, u32[]{:S(2)}, u32[]{:S(2)}) %collective-permute-start.5) | collective-permute-done | bytes 2097184 | tf_op jit(solution)/shard_map/ppermute | solution.py:8
  342.0 6.3 %bitcast_convert_fusion = bf16[4,256,1024]{2,1,0:T(8,128)(2,1)} fusion(bf16[4,4,256,256]{3,2,1,0:T(8,128)(2,1)} %all-gather.5.cloned.1.call-done, bf16[1,4,256,1024]{3,2,1,0:T(8,128)(2,1)} %bitcast.17, bf16[1,4,256,1024]{3,2,1,0:T(8,128)(2,1)} %bitcast.16, bf16[1,4,256,1024]{3,2,1,0:T(8,128)(2,1)} %bitcast.15, bf16[1,4,256,1024]{3,2,1,0:T(8,128)(2,1)} %bitcast.14), kind=kOutput, calls=%fused_computation.8 | convolution fusion | flops 2161115136 | bytes 12582912 | tf_op jit(solution)/shard_map/lers,elsc->lrc/dot_general | solution.py:28
  (6 shorter events, 0.0 us)
Async XLA Ops:
  6.5 39.8 %copy-start = (bf16[4,256,1024]{2,1,0:T(8,128)(2,1)S(1)}, bf16[4,256,1024]{2,1,0:T(8,128)(2,1)}, u32[]{:S(2)}) copy-start(bf16[4,256,1024]{2,1,0:T(8,128)(2,1)} %param.4) | copy-start | bytes 6291460
  6.5 39.8 %all-gather.9.cloned.1.call-start = ((), (), s32[]{:S(2)}) async-start(), calls=%async_computation.2 | async-start | bytes 3145728 | tf_op jit(solution)/shard_map/all_gather | solution.py:30
  10.3 77.7 %all-gather.7.cloned.1.call-start = ((), (), s32[]{:S(2)}) async-start(), calls=%async_computation.1 | async-start | bytes 3145728 | tf_op jit(solution)/shard_map/all_gather | solution.py:30
  51.6 4.6 %collective-permute-start = (bf16[4,256,1024]{2,1,0:T(8,128)(2,1)}, bf16[4,256,1024]{2,1,0:T(8,128)(2,1)}, u32[]{:S(2)}, u32[]{:S(2)}) collective-permute-start(bf16[4,256,1024]{2,1,0:T(8,128)(2,1)} %bitcast_convert_fusion.2), channel_id=1, source_target_pairs={{0,2},{2,0},{4,6},{6,4},{8,10},{10,8},{12,14},{14,12},{16,18},{18,... | collective-permute-start | bytes 6291464 | tf_op jit(solution)/shard_map/ppermute | solution.py:8
  54.6 189.4 %all-gather.5.cloned.1.call-start = ((), (), s32[]{:S(2)}) async-start(), calls=%async_computation | async-start | bytes 3145728 | tf_op jit(solution)/shard_map/all_gather | solution.py:30
  54.6 48.9 %collective-permute-start.1 = (bf16[4,256,1024]{2,1,0:T(8,128)(2,1)}, bf16[4,256,1024]{2,1,0:T(8,128)(2,1)}, u32[]{:S(2)}, u32[]{:S(2)}) collective-permute-start(bf16[4,256,1024]{2,1,0:T(8,128)(2,1)} %bitcast_convert_fusion.2), channel_id=1, source_target_pairs={{0,4},{2,6},{4,0},{6,2},{8,12},{10,14},{12,8},{14,10},{16,20},{18,... | collective-permute-start | bytes 6291464 | tf_op jit(solution)/shard_map/ppermute | solution.py:8
  56.2 91.8 %collective-permute-start.2 = (bf16[4,256,1024]{2,1,0:T(8,128)(2,1)}, bf16[4,256,1024]{2,1,0:T(8,128)(2,1)}, u32[]{:S(2)}, u32[]{:S(2)}) collective-permute-start(bf16[4,256,1024]{2,1,0:T(8,128)(2,1)} %collective-permute-done), channel_id=1, source_target_pairs={{0,4},{2,6},{4,0},{6,2},{8,12},{10,14},{12,8},{14,10},{16,20},{18,... | collective-permute-start | bytes 6291464 | tf_op jit(solution)/shard_map/ppermute | solution.py:8
  154.4 89.1 %collective-permute-start.3 = (bf16[4,256,1024]{2,1,0:T(8,128)(2,1)}, bf16[4,256,1024]{2,1,0:T(8,128)(2,1)}, u32[]{:S(2)}, u32[]{:S(2)}) collective-permute-start(bf16[4,256,1024]{2,1,0:T(8,128)(2,1)} %bitcast_convert_fusion.1), channel_id=1, source_target_pairs={{0,8},{2,10},{4,12},{6,14},{8,0},{10,2},{12,4},{14,6},{16,24},{18,... | collective-permute-start | bytes 6291464 | tf_op jit(solution)/shard_map/ppermute | solution.py:8
  158.9 139.7 %collective-permute-start.4 = (bf16[4,256,1024]{2,1,0:T(8,128)(2,1)}, bf16[4,256,1024]{2,1,0:T(8,128)(2,1)}, u32[]{:S(2)}, u32[]{:S(2)}) collective-permute-start(bf16[4,256,1024]{2,1,0:T(8,128)(2,1)} %bitcast_convert_fusion.1), channel_id=1, source_target_pairs={{0,16},{2,18},{4,20},{6,22},{8,24},{10,26},{12,28},{14,30},{16,0},... | collective-permute-start | bytes 6291464 | tf_op jit(solution)/shard_map/ppermute | solution.py:8
  243.5 98.4 %collective-permute-start.5 = (bf16[4,256,1024]{2,1,0:T(8,128)(2,1)}, bf16[4,256,1024]{2,1,0:T(8,128)(2,1)}, u32[]{:S(2)}, u32[]{:S(2)}) collective-permute-start(bf16[4,256,1024]{2,1,0:T(8,128)(2,1)} %collective-permute-done.3), channel_id=1, source_target_pairs={{0,16},{2,18},{4,20},{6,22},{8,24},{10,26},{12,28},{14,30},{16,0},... | collective-permute-start | bytes 6291464 | tf_op jit(solution)/shard_map/ppermute | solution.py:8
Sparse Core Ops, SparseCore 0:
  10.5 35.8 all-gather.8
  54.7 33.2 all-gather.6
  159.0 32.1 all-gather.4
where the time goes:
time: 355 us
  waiting for transfers between devices  307 us (86%)
  matrix products  17.9 us (5%)
  between operations  13.1 us (4%)
  local copies, waits for them, and re-layouts  7.45 us (2%)
  starting transfers between devices  7.39 us (2%)
    ppermute x6, waiting for transfers between devices, from_partner(): lax.ppermute(array, axis, [(i, i ^ 1 << apart) for i in range(lax.axis_si...  240 us
    all_gather x3, waiting for transfers between devices, local(): lax.all_gather(weights_now, 'col', axis=2, tiled=True)  66.4 us
    dot_general x3, matrix products, local(): jnp.einsum(form, lax.all_gather(weights_now, 'col', axis=2, tiled=True),...  17.9 us
    ppermute x6, starting transfers between devices, from_partner(): lax.ppermute(array, axis, [(i, i ^ 1 << apart) for i in range(lax.axis_si...  7.3 us
  transfers between devices with their start and end apart: 9, of which 7 were waited for; matrix products, arithmetic and copies ran while one was open for 2% of the time, Pallas kernels for 0%

commit v1 on v0

v1 whole, which is shorter than its diff:
```python
import functools

import jax
import jax.numpy as jnp
from jax import lax
from jax.experimental import pallas as pl
from jax.experimental.pallas import tpu as pltpu
from jax.sharding import PartitionSpec as P

MESH = pl.DeviceIdType.MESH
WIDTH = 256
LAG_FORWARD, LAG_ONE, LAG_RELAY, LAG_FAR, LAG_MID, LAG_END = 1, 2, 3, 4, 6, 8
TO_CORE, TO_TWO, FORWARD, TO_PAIR, TO_ACROSS, RELAY, PARTIAL = range(7)


def flip(i, bit):
    return i + bit - 2 * bit * (i // bit % 2)


def dot(a, b):
    return jnp.dot(a, b, preferred_element_type=jnp.float32)


def kernel(
    cols, chunks, x_in, t_in, out_ref,
    x, t, t_far, y0, near, y1, pair, across, relayed, partial_out, partial_in, out_buf,
    x_sem, t_sem, out_sem, send, recv, t_send, t_recv, far_send, far_recv,
):
    nodes_here = x_in.shape[0]
    rows = t_in.shape[3]
    units = nodes_here * chunks
    width = x_in.shape[2] // chunks
    me = lax.axis_index("node")
    my_col = lax.axis_index("col")
    one = me % 4
    two = me // 4 % 4
    is_mid = (two + 1) // 2 % 2 == 1
    is_end = (two + 1) // 2 % 2 == 0
    by_core, by_two, by_pair = flip(me, 1), flip(me, 2), flip(me, 4)
    by_across = flip(flip(me, 4), 8)

    x_copy = pltpu.make_async_copy(x_in, x, x_sem)
    x_copy.start()
    t_copy = pltpu.make_async_copy(t_in, t.at[:, :, :, pl.ds(my_col * rows, rows), :], t_sem)
    t_copy.start()

    barrier = pltpu.get_barrier_semaphore()
    for other in (by_core, by_two, by_pair):
        pl.semaphore_signal(barrier, inc=1, device_id={"node": other}, device_id_type=MESH)
    for k in range(1, cols):
        pl.semaphore_signal(barrier, inc=1, device_id={"col": (my_col + k) % cols}, device_id_type=MESH)

    @pl.when(is_mid)
    def _():
        pl.semaphore_signal(barrier, inc=1, device_id={"node": by_across}, device_id_type=MESH)
        pl.semaphore_wait(barrier, 4 + cols - 1)

    @pl.when(is_end)
    def _():
        pl.semaphore_wait(barrier, 3 + cols - 1)

    def t_rows(level, m, k):
        return pltpu.make_async_remote_copy(
            src_ref=t_in.at[level, m],
            dst_ref=t.at[level, m, :, pl.ds(my_col * rows, rows), :],
            send_sem=t_send.at[level, m, k - 1],
            recv_sem=t_recv.at[level, m, k - 1],
            device_id={"col": (my_col + k) % cols},
            device_id_type=MESH,
        )

    def wait_rows(level, m):
        for k in range(1, cols):
            source = (my_col + cols - k) % cols
            pltpu.make_async_remote_copy(
                src_ref=t_in.at[level, m],
                dst_ref=t.at[level, m, :, pl.ds(source * rows, rows), :],
                send_sem=t_send.at[level, m, k - 1],
                recv_sem=t_recv.at[level, m, k - 1],
                device_id={"col": (my_col + k) % cols},
                device_id_type=MESH,
            ).wait_recv()

    for m in range(nodes_here):
        for level in range(3):
            for k in range(1, cols):
                t_rows(level, m, k).start()

    routes = {
        TO_CORE: (y0, near.at[0], by_core),
        TO_TWO: (y0, near.at[1], by_two),
        FORWARD: (near.at[1], near.at[2], by_core),
        TO_PAIR: (y1, pair, by_pair),
        TO_ACROSS: (y1, across, by_across),
        RELAY: (pair, relayed, by_across),
        PARTIAL: (partial_out, partial_in, by_pair),
    }

    def copy(kind, u):
        source, target, device = routes[kind]
        return pltpu.make_async_remote_copy(
            src_ref=source.at[u],
            dst_ref=target.at[u],
            send_sem=send.at[kind, u],
            recv_sem=recv.at[kind, u],
            device_id={"node": device},
            device_id_type=MESH,
        )

    def far(m, i):
        return pltpu.make_async_remote_copy(
            src_ref=t.at[2, m, flip(two, 2) if i == 0 else 3 - two],
            dst_ref=t_far.at[m, i],
            send_sem=far_send.at[m, i],
            recv_sem=far_recv.at[m, i],
            device_id={"node": by_pair},
            device_id_type=MESH,
        )

    def out_copy(u):
        columns = pl.ds(pl.multiple_of(u % chunks * width, width), width)
        return pltpu.make_async_copy(out_buf.at[u], out_ref.at[u // chunks, :, columns], out_sem.at[u])

    def first(u, action):
        @pl.when(u % chunks == 0)
        def _():
            action(u // chunks)

    def stage_zero(u):
        first(u, lambda m: wait_rows(0, m))
        m = u // chunks
        columns = pl.ds(pl.multiple_of(u % chunks * width, width), width)
        total = dot(t[0, m, 0], x[0, :, columns])
        for j in range(1, 4):
            total += dot(t[0, m, j], x[j, :, columns])
        y0[u] = total.astype(y0.dtype)
        copy(TO_TWO, u).start()
        copy(TO_CORE, u).start()

    def stage_forward(u):
        copy(TO_TWO, u).wait_recv()
        copy(FORWARD, u).start()

    def stage_one(u):
        first(u, lambda m: wait_rows(1, m))
        m = u // chunks
        copy(TO_CORE, u).wait_recv()
        copy(FORWARD, u).wait_recv()
        total = dot(t[1, m, one], y0[u])
        total += dot(t[1, m, flip(one, 1)], near[0, u])
        total += dot(t[1, m, flip(one, 2)], near[1, u])
        total += dot(t[1, m, 3 - one], near[2, u])
        y1[u] = total.astype(y1.dtype)

        @pl.when(is_mid)
        def _():
            copy(TO_ACROSS, u).start()

        copy(TO_PAIR, u).start()

    def stage_relay(u):
        copy(TO_PAIR, u).wait_recv()
        copy(RELAY, u).start()

    def stage_far(u):
        def send_far(m):
            wait_rows(2, m)
            far(m, 0).start()
            far(m, 1).start()

        first(u, send_far)

    def stage_mid(u):
        def arrive(m):
            wait_rows(2, m)
            far(m, 0).wait_recv()
            far(m, 1).wait_recv()

        first(u, arrive)
        m = u // chunks
        copy(TO_ACROSS, u).wait_recv()
        copy(RELAY, u).wait_recv()
        part = dot(t_far[m, 0], across[u]) + dot(t_far[m, 1], relayed[u])
        partial_out[u] = part.astype(partial_out.dtype)
        copy(PARTIAL, u).start()
        total = dot(t[2, m, two], y1[u])
        total += dot(t[2, m, flip(two, 1)], pair[u])
        total += dot(t[2, m, 3 - two], across[u])
        total += dot(t[2, m, flip(two, 2)], relayed[u])
        out_buf[u] = total.astype(out_buf.dtype)
        out_copy(u).start()

    def stage_end(u):
        m = u // chunks
        copy(TO_PAIR, u).wait_recv()
        total = dot(t[2, m, two], y1[u]) + dot(t[2, m, flip(two, 1)], pair[u])
        copy(PARTIAL, u).wait_recv()
        out_buf[u] = (total + partial_in[u].astype(jnp.float32)).astype(out_buf.dtype)
        out_copy(u).start()

    x_copy.wait()
    t_copy.wait()

    def step(s, _):
        def run(stage, lag, role=None):
            u = s - lag
            ready = (u >= 0) & (u < units)

            @pl.when(ready if role is None else ready & role)
            def _():
                stage(u)

        run(stage_forward, LAG_FORWARD)
        run(stage_one, LAG_ONE)
        run(stage_relay, LAG_RELAY, is_mid)
        run(stage_far, LAG_FAR, is_end)
        run(stage_mid, LAG_MID, is_mid)
        run(stage_end, LAG_END, is_end)
        run(stage_zero, 0)
        return 0

    lax.fori_loop(0, units + LAG_END, step, 0)

    def drain(u, _):
        for kind in (TO_CORE, TO_TWO, FORWARD, TO_PAIR):
            copy(kind, u).wait_send()

        @pl.when(is_mid)
        def _():
            for kind in (TO_ACROSS, RELAY, PARTIAL):
                copy(kind, u).wait_send()

        out_copy(u).wait()
        return 0

    lax.fori_loop(0, units, drain, 0)

    def drain_rows(m, _):
        for level in range(3):
            for k in range(1, cols):
                t_rows(level, m, k).wait_send()

        @pl.when(is_end)
        def _():
            far(m, 0).wait_send()
            far(m, 1).wait_send()

        return 0

    lax.fori_loop(0, nodes_here, drain_rows, 0)


def local(coefficients, transfer):
    cols = lax.axis_size("col")
    nodes_here, rank, columns = coefficients.shape
    levels, _, children, rows, _ = transfer.shape
    width = min(WIDTH, columns)
    chunks = columns // width
    units = nodes_here * chunks
    kind = coefficients.dtype
    block = (units, rank, width)
    return pl.pallas_call(
        functools.partial(kernel, cols, chunks),
        out_shape=jax.ShapeDtypeStruct(coefficients.shape, kind),
        in_specs=[pl.BlockSpec(memory_space=pl.ANY)] * 2,
        out_specs=pl.BlockSpec(memory_space=pl.ANY),
        scratch_shapes=[
            pltpu.VMEM(coefficients.shape, kind),
            pltpu.VMEM((levels, nodes_here, children, rank, rank), kind),
            pltpu.VMEM((nodes_here, 2, rank, rank), kind),
            pltpu.VMEM(block, kind),
            pltpu.VMEM((3,) + block, kind),
            pltpu.VMEM(block, kind),
            pltpu.VMEM(block, kind),
            pltpu.VMEM(block, kind),
            pltpu.VMEM(block, kind),
            pltpu.VMEM(block, kind),
            pltpu.VMEM(block, kind),
            pltpu.VMEM(block, kind),
            pltpu.SemaphoreType.DMA,
            pltpu.SemaphoreType.DMA,
            pltpu.SemaphoreType.DMA((units,)),
            pltpu.SemaphoreType.DMA((7, units)),
            pltpu.SemaphoreType.DMA((7, units)),
            pltpu.SemaphoreType.DMA((levels, nodes_here, max(cols - 1, 1))),
            pltpu.SemaphoreType.DMA((levels, nodes_here, max(cols - 1, 1))),
            pltpu.SemaphoreType.DMA((nodes_here, 2)),
            pltpu.SemaphoreType.DMA((nodes_here, 2)),
        ],
        compiler_params=pltpu.CompilerParams(
            collective_id=0, has_side_effects=True, vmem_limit_bytes=56 * 1024 * 1024
        ),
    )(coefficients, transfer)


def solution(mesh):
    return jax.shard_map(
        local,
        mesh=mesh,
        in_specs=(P("node", None, "col"), P(None, "node", None, "col", None)),
        out_specs=P("node", None, "col"),
        check_vma=False,
    )
```

time: 355 us -> 133 us (0.37)
  waiting for transfers between devices: 307 us -> 0 us
  Pallas kernels: 0 us -> 130 us
  matrix products: 17.9 us -> 0 us
  between operations: 13.1 us -> 0.01 us
  starting transfers between devices: 7.39 us -> 0 us
  local copies, waits for them, and re-layouts: 7.45 us -> 3.08 us
    ppermute x6 -> x0, waiting for transfers between devices: 240 us -> none  [from_partner(): lax.ppermute(array, axis, [(i, i ^ 1 << apart) for i in range(lax.axis_si...]
    pallas_call x0 -> x1, Pallas kernels: none -> 130 us  [local(): pl.pallas_call(functools.partial(kernel, cols, chunks), out_shape=jax.Sha...]
    all_gather x3 -> x0, waiting for transfers between devices: 66.4 us -> none  [local(): lax.all_gather(weights_now, 'col', axis=2, tiled=True)]
    dot_general x3 -> x0, matrix products: 17.9 us -> none  [local(): jnp.einsum(form, lax.all_gather(weights_now, 'col', axis=2, tiled=True),...]
    ppermute x6 -> x0, starting transfers between devices: 7.3 us -> none  [from_partner(): lax.ppermute(array, axis, [(i, i ^ 1 << apart) for i in range(lax.axis_si...]
    slice x1 -> x0, local copies, waits for them, and re-layouts: 3.77 us -> none  [local(): weights_now = transfer[level_index]]
    gather x2 -> x0, local copies, waits for them, and re-layouts: 3.67 us -> none  [local(): weights_now = jnp.take(weights_now, order_idx, axis=1)]
  transfers between devices with their start and end apart: 9 -> 0, of which waited for: 7 -> 0; matrix products, arithmetic and copies ran while one was open for 2% -> 0% of each run, Pallas kernels for 0% -> 0%
where the time goes in v1:
time: 133 us
  Pallas kernels  130 us (98%)
  local copies, waits for them, and re-layouts  3.08 us (2%)
    pallas_call x1, Pallas kernels, local(): pl.pallas_call(functools.partial(kernel, cols, chunks), out_shape=jax.Sha...  130 us
    unnamed x1, local copies, waits for them, and re-layouts  3.08 us

profile of v1, /device:TPU:0, one launch (start us, length us, event | category | flops | bytes accessed | tf_op | source)
XLA Modules:
  0.0 133.2 jit_solution(8938537587757202076)
XLA Ops:
  0.0 130.1 %shard_map.28 = bf16[4,256,1024]{2,1,0:T(8,128)(2,1)} custom-call(bf16[4,256,1024]{2,1,0:T(8,128)(2,1)} %x_in.1, bf16[3,4,4,128,256]{4,3,2,1,0:T(8,128)(2,1)} %t_in.1), custom_call_target="tpu_custom_call" | custom-call | tf_op jit(solution)/shard_map/pallas_call | solution.py:262
  130.1 3.1 %copy.4 = bf16[4,256,1024]{2,1,0:T(8,128)(2,1)} copy(bf16[4,256,1024]{2,1,0:T(8,128)(2,1)} %shard_map.28) | data formatting | bytes 4194304

commit v2 on v1

--- a/solution.py
+++ b/solution.py
@@ -9,7 +9,7 @@
 
 MESH = pl.DeviceIdType.MESH
 WIDTH = 256
-LAG_FORWARD, LAG_ONE, LAG_RELAY, LAG_FAR, LAG_MID, LAG_END = 1, 2, 3, 4, 6, 8
+LAG_FORWARD, LAG_ONE, LAG_RELAY, LAG_FAR, LAG_MID, LAG_END = 2, 4, 6, 5, 9, 11
 TO_CORE, TO_TWO, FORWARD, TO_PAIR, TO_ACROSS, RELAY, PARTIAL = range(7)
 
 
@@ -81,10 +81,10 @@
                 device_id_type=MESH,
             ).wait_recv()
 
-    for m in range(nodes_here):
-        for level in range(3):
-            for k in range(1, cols):
-                t_rows(level, m, k).start()
+    order = sorted((2 * m + (0, 1, 3)[level], level, m) for m in range(nodes_here) for level in range(3))
+    for _, level, m in order:
+        for k in range(1, cols):
+            t_rows(level, m, k).start()
 
     routes = {
         TO_CORE: (y0, near.at[0], by_core),

time: 133 us -> 126 us (0.947)
  Pallas kernels: 130 us -> 122 us
    pallas_call x1, Pallas kernels: 130 us -> 122 us  [local(): pl.pallas_call(functools.partial(kernel, cols, chunks), out_shape=jax.Sha...]
where the time goes in v2:
time: 126 us
  Pallas kernels  122 us (97%)
  local copies, waits for them, and re-layouts  3.08 us (2%)
    pallas_call x1, Pallas kernels, local(): pl.pallas_call(functools.partial(kernel, cols, chunks), out_shape=jax.Sha...  122 us
    unnamed x1, local copies, waits for them, and re-layouts  3.08 us

profile of v2, /device:TPU:0, one launch (start us, length us, event | category | flops | bytes accessed | tf_op | source)
XLA Modules:
  0.0 125.6 jit_solution(9864118388233190425)
XLA Ops:
  0.0 122.5 %shard_map.28 = bf16[4,256,1024]{2,1,0:T(8,128)(2,1)} custom-call(bf16[4,256,1024]{2,1,0:T(8,128)(2,1)} %x_in.1, bf16[3,4,4,128,256]{4,3,2,1,0:T(8,128)(2,1)} %t_in.1), custom_call_target="tpu_custom_call" | custom-call | tf_op jit(solution)/shard_map/pallas_call | solution.py:262
  122.5 3.1 %copy.4 = bf16[4,256,1024]{2,1,0:T(8,128)(2,1)} copy(bf16[4,256,1024]{2,1,0:T(8,128)(2,1)} %shard_map.28) | data formatting | bytes 4194304

commit v3 on v2

--- a/solution.py
+++ b/solution.py
@@ -9,7 +9,7 @@
 
 MESH = pl.DeviceIdType.MESH
 WIDTH = 256
-LAG_FORWARD, LAG_ONE, LAG_RELAY, LAG_FAR, LAG_MID, LAG_END = 2, 4, 6, 5, 9, 11
+LAG_FORWARD, LAG_ONE, LAG_RELAY, LAG_FAR, LAG_MID, LAG_END = 2, 4, 7, 5, 9, 11
 TO_CORE, TO_TWO, FORWARD, TO_PAIR, TO_ACROSS, RELAY, PARTIAL = range(7)
 
 

time: 126 us -> 125 us (level)
  no operation moved by 1% of the time
where the time goes in v3:
time: 125 us
  Pallas kernels  122 us (98%)
  local copies, waits for them, and re-layouts  3.08 us (2%)
    pallas_call x1, Pallas kernels, local(): pl.pallas_call(functools.partial(kernel, cols, chunks), out_shape=jax.Sha...  122 us
    unnamed x1, local copies, waits for them, and re-layouts  3.08 us

profile of v3, /device:TPU:0, one launch (start us, length us, event | category | flops | bytes accessed | tf_op | source)
XLA Modules:
  0.0 124.7 jit_solution(8072542554705483676)
XLA Ops:
  0.0 121.6 %shard_map.28 = bf16[4,256,1024]{2,1,0:T(8,128)(2,1)} custom-call(bf16[4,256,1024]{2,1,0:T(8,128)(2,1)} %x_in.1, bf16[3,4,4,128,256]{4,3,2,1,0:T(8,128)(2,1)} %t_in.1), custom_call_target="tpu_custom_call" | custom-call | tf_op jit(solution)/shard_map/pallas_call | solution.py:262
  121.6 3.1 %copy.4 = bf16[4,256,1024]{2,1,0:T(8,128)(2,1)} copy(bf16[4,256,1024]{2,1,0:T(8,128)(2,1)} %shard_map.28) | data formatting | bytes 4194304
